TPU v7x, 256 devices: a 8x8x2 block of a 8x8x16 slice. The times are simulated.
256 devices in a mesh: groups: 2 (over z), rows: 16 (over y, core), cols: 8 (over x).
Axes of the slice: x: 8, y: 8, z: 2, core: 2. Of those that a mesh axis runs over, the one named last changes fastest.
The devices are a block of a 8x8x16 slice.
Arguments:
- pair_state: float32 [768, 384, 128], P(('groups', 'rows'), 'cols'), parts along dimension 0, may hold values from -6 to 6
- token_mask: int32 [768], P('groups'), parts along dimension 0, may hold values 0 or 1
- norm_gain: float32 [2, 128], replicated, may hold values from 0.25 to 1.75
- norm_bias: float32 [2, 128], replicated, may hold values from -3 to 3
- proj_weight: float32 [2, 128, 512], replicated, may hold values from -0.5 to 0.5
- gate_weight: float32 [2, 128, 128], replicated, may hold values from -0.5 to 0.5
- out_gain: float32 [2, 128], replicated, may hold values from 0.25 to 1.75
- out_bias: float32 [2, 128], replicated, may hold values from -3 to 3
- out_weight: float32 [2, 128, 128], replicated, may hold values from -0.5 to 0.5
Outputs:
- pair_out: float32 [768, 384, 128], P(('groups', 'rows'), 'cols'), parts along dimension 0
There are 2 independent parts, one for each index of `groups`. A program takes and returns all parts, laid end to end along the dimension named above; an argument that names none is the same for every part. Nothing has to cross between parts.
All inputs are finite; a program needn't handle non-finite values.
Results may differ from a plain program's by a relative error of at most 0.0001.
Values sent between devices are 32-bit elements; how exact they have to be, the bound alone decides.
A program may use at most 128 MiB of HBM per device.

v0:
```python
import jax
import jax.numpy as jnp
from jax import lax
from jax.sharding import PartitionSpec as P

eps = 1e-05


def normalize(values, gain, shift):
    center = values - jnp.mean(values, axis=-1, keepdims=True)
    spread = jnp.mean(center * center, axis=-1, keepdims=True)
    return center * lax.rsqrt(spread + eps) * gain + shift


def project(state, pair_mask, segment, norm_gain, norm_bias, proj_weight, gate_weight):
    width = proj_weight.shape[2] // 4
    normed = normalize(state, norm_gain[segment], norm_bias[segment])
    hidden = jnp.einsum(
        "ijc,cf->ijf", normed, proj_weight[segment], precision=lax.Precision.HIGHEST
    )
    left_side = (
        pair_mask[:, :, None]
        * jax.nn.sigmoid(hidden[:, :, :width])
        * hidden[:, :, width : 2 * width]
    )
    right_side = (
        pair_mask[:, :, None]
        * jax.nn.sigmoid(hidden[:, :, 2 * width : 3 * width])
        * hidden[:, :, 3 * width :]
    )
    gating = jax.nn.sigmoid(
        jnp.einsum("ijc,cd->ijd", normed, gate_weight[segment], precision=lax.Precision.HIGHEST)
    )
    return (left_side, right_side, gating)


def finish(state, mixed, gating, segment, out_gain, out_bias, out_weight):
    result = jnp.einsum(
        "ijh,hc->ijc",
        normalize(mixed, out_gain[segment], out_bias[segment]),
        out_weight[segment],
        precision=lax.Precision.HIGHEST,
    )
    return state + gating * result


def body(
    pair_state,
    token_mask,
    norm_gain,
    norm_bias,
    proj_weight,
    gate_weight,
    out_gain,
    out_bias,
    out_weight,
):
    row_count = pair_state.shape[0]
    col_count = pair_state.shape[1]
    row_start = lax.axis_index("rows") * row_count
    col_start = lax.axis_index("cols") * col_count
    maskf = token_mask.astype(jnp.float32)
    row_mask = lax.dynamic_slice_in_dim(maskf, row_start, row_count)
    col_mask = lax.dynamic_slice_in_dim(maskf, col_start, col_count)
    pair_mask = row_mask[:, None] * col_mask[None, :]
    left_side, right_side, gating = project(
        pair_state, pair_mask, 0, norm_gain, norm_bias, proj_weight, gate_weight
    )
    partial_out = jnp.einsum(
        "ikh,jkh->ijh",
        left_side,
        lax.all_gather(right_side, "rows", axis=0, tiled=True),
        precision=lax.Precision.HIGHEST,
    )
    mixed = lax.psum_scatter(partial_out, "cols", scatter_dimension=1, tiled=True)
    updated = finish(pair_state, mixed, gating, 0, out_gain, out_bias, out_weight)
    left_next, right_next, gate_next = project(
        updated, pair_mask, 1, norm_gain, norm_bias, proj_weight, gate_weight
    )
    partial_in = jnp.einsum(
        "kih,kjh->ijh",
        lax.all_gather(left_next, "cols", axis=1, tiled=True),
        right_next,
        precision=lax.Precision.HIGHEST,
    )
    mixed_next = lax.psum_scatter(partial_in, "rows", scatter_dimension=0, tiled=True)
    return finish(updated, mixed_next, gate_next, 1, out_gain, out_bias, out_weight)


def solution(mesh):
    placed = (P(("groups", "rows"), "cols", None), P("groups"), P(), P(), P(), P(), P(), P(), P())
    return jax.shard_map(
        body,
        mesh=mesh,
        in_specs=placed,
        out_specs=P(("groups", "rows"), "cols", None),
        check_vma=False,
    )
```

profile of v0, /device:TPU:513, one launch (start us, length us, event | category | flops | bytes accessed | tf_op | source)
XLA Modules:
  0.0 395.3 jit_solution(2512777455134591097)
XLA Ops:
  6.6 0.7 convert_element_type.3
  7.2 0.1 dynamic_slice.6
  7.3 0.1 dynamic_slice.7
  7.4 1.3 reduce_sum.72
  8.7 1.5 multiply_reduce_fusion.3
  10.2 0.1 broadcast_multiply_fusion
  10.3 0.8 slice_bitcast_fusion.2
  11.0 3.2 fusion.29
  14.2 1.2 slice_multiply_fusion.2
  15.4 0.1 all-gather.3.cloned.1.call-update
  15.4 0.1 reduce-scatter.3.cloned.1.call-start
  15.5 0.5 copy.47
  16.1 80.9 %all-gather.3.cloned.1.call-done = f32[384,48,128]{2,1,0:T(8,128)} async-done(((f32[24,48,128]{2,1,0:T(8,128)}), f32[384,48,128]{2,1,0:T(8,128)}) %all-gather.3.cloned.1.call-update) | async-done | bytes 9437200 | tf_op jit(solution)/shard_map/all_gather | solution.py:72
  96.9 21.7 %copy.46 = f32[384,48,128]{1,0,2:T(8,128)} copy(f32[384,48,128]{2,1,0:T(8,128)} %all-gather.3.cloned.1.call-done) | data formatting | bytes 18874368 | tf_op jit(solution)/shard_map/all_gather | solution.py:72
  118.6 31.6 %convolution_bitcast_fusion.1 = f32[24,384,128]{1,0,2:T(8,128)} fusion(f32[384,48,128]{1,0,2:T(8,128)} %copy.46, f32[24,48,128]{1,0,2:T(8,128)S(1)} %copy.47), kind=kOutput, calls=%fused_computation.1 | convolution fusion | flops 679477248 | bytes 14745600 | tf_op jit(solution)/shard_map/ikh,jkh->ijh/dot_general | solution.py:69
  150.2 6.0 %copy.48 = f32[24,384,128]{2,0,1:T(8,128)} copy(f32[24,384,128]{1,0,2:T(8,128)} %convolution_bitcast_fusion.1) | data formatting | bytes 9437184 | tf_op jit(solution)/shard_map/ikh,jkh->ijh/transpose | solution.py:69
  156.2 0.1 reduce-scatter.3.cloned.1.call-update
  156.3 0.2 all-gather.5.cloned.1.call-start
  156.6 0.3 copy-done.3
  156.9 0.0 copy-done.4
  156.9 0.4 copy-done
  157.3 0.0 copy-done.5
  157.3 0.8 fusion.7
  158.1 57.7 %reduce-scatter.3.cloned.1.call-done = f32[24,48,128]{2,0,1:T(8,128)} async-done(((f32[24,384,128]{2,0,1:T(8,128)}), f32[24,48,128]{2,0,1:T(8,128)}) %reduce-scatter.3.cloned.1.call-update) | async-done | bytes 589840 | tf_op jit(solution)/shard_map/reduce_scatter | solution.py:75
  215.8 1.3 reduce_sum.74
  217.1 0.1 copy.49
  217.2 0.1 copy.50
  217.3 1.5 multiply_reduce_fusion.2
  218.7 0.1 copy.51
  218.8 0.1 copy.52
  218.9 1.4 multiply_add_fusion.1
  220.4 0.7 fusion.63
  221.1 0.4 multiply_reduce_fusion.1
  221.5 2.1 fusion.30
  223.6 1.2 slice_multiply_fusion
  224.8 0.1 all-gather.5.cloned.1.call-update
  224.8 0.1 reduce-scatter.5.cloned.1.call-start
  224.9 0.5 copy.54
  225.4 59.2 %all-gather.5.cloned.1.call-done = f32[24,384,128]{2,1,0:T(8,128)} async-done(((f32[24,48,128]{2,1,0:T(8,128)}), f32[24,384,128]{2,1,0:T(8,128)}) %all-gather.5.cloned.1.call-update) | async-done | bytes 4718608 | tf_op jit(solution)/shard_map/all_gather | solution.py:82
  284.6 6.2 %copy.55 = f32[24,384,128]{1,0,2:T(8,128)} copy(f32[24,384,128]{2,1,0:T(8,128)} %all-gather.5.cloned.1.call-done) | data formatting | bytes 9437184 | tf_op jit(solution)/shard_map/all_gather | solution.py:82
  290.8 11.8 %convolution_bitcast_fusion = f32[384,48,128]{0,1,2:T(8,128)} fusion(f32[24,48,128]{1,0,2:T(8,128)S(1)} %copy.54, f32[24,384,128]{1,0,2:T(8,128)} %copy.55), kind=kOutput, calls=%fused_computation | convolution fusion | flops 679477248 | bytes 14745600 | tf_op jit(solution)/shard_map/kih,kjh->ijh/dot_general | solution.py:80
  302.6 9.8 %copy.56 = f32[384,48,128]{2,1,0:T(8,128)} copy(f32[384,48,128]{0,1,2:T(8,128)} %convolution_bitcast_fusion) | data formatting | bytes 18874368 | tf_op jit(solution)/shard_map/kih,kjh->ijh/transpose | solution.py:80
  312.4 0.1 reduce-scatter.5.cloned.1.call-update
  312.4 0.8 fusion.3
  313.2 70.0 %reduce-scatter.5.cloned.1.call-done = f32[24,48,128]{2,1,0:T(8,128)} async-done(((f32[384,48,128]{2,1,0:T(8,128)}), f32[24,48,128]{2,1,0:T(8,128)}) %reduce-scatter.5.cloned.1.call-update) | async-done | bytes 589840 | tf_op jit(solution)/shard_map/reduce_scatter | solution.py:86
  383.3 1.3 reduce_sum.78
  384.6 1.5 multiply_reduce_fusion
  386.1 2.7 fusion
  (18 shorter events, 0.1 us)
Async XLA Ops:
  6.5 90.4 %all-gather.3.cloned.1.call-start = ((), (), s32[]{:S(2)}) async-start(), calls=%async_computation.2 | async-start | bytes 10027008 | tf_op jit(solution)/shard_map/all_gather | solution.py:72
  15.4 200.4 %reduce-scatter.3.cloned.1.call-start = ((), (), s32[]{:S(2)}) async-start(), calls=%async_computation.3 | async-start | bytes 5308416 | tf_op jit(solution)/shard_map/reduce_scatter | solution.py:75
  156.2 0.7 copy-start.3
  156.2 0.7 copy-start.4
  156.2 1.1 copy-start
  156.2 1.1 copy-start.5
  156.2 64.1 %copy-start.2 = (f32[2,128,128]{2,1,0:T(8,128)S(1)}, f32[2,128,128]{2,1,0:T(8,128)}, u32[]{:S(2)}) copy-start(f32[2,128,128]{2,1,0:T(8,128)} %param.17) | copy-start | bytes 393220
  156.3 65.2 %copy-start.1 = (f32[2,128,512]{2,1,0:T(8,128)S(1)}, f32[2,128,512]{2,1,0:T(8,128)}, u32[]{:S(2)}) copy-start(f32[2,128,512]{2,1,0:T(8,128)} %param.13) | copy-start | bytes 1572868
  156.3 128.3 %all-gather.5.cloned.1.call-start = ((), (), s32[]{:S(2)}) async-start(), calls=%async_computation.4 | async-start | bytes 5308416 | tf_op jit(solution)/shard_map/all_gather | solution.py:82
  224.8 158.5 %reduce-scatter.5.cloned.1.call-start = ((), (), s32[]{:S(2)}) async-start(), calls=%async_computation.5 | async-start | bytes 10027008 | tf_op jit(solution)/shard_map/reduce_scatter | solution.py:86
Sparse Core Ops, SparseCore 0:
  15.6 81.3 all-gather.2
  156.4 59.3 reduce-scatter.2
  224.9 59.6 all-gather.4
  312.5 70.6 reduce-scatter.4
where the time goes:
time: 398 us; the launch traced here: 395 us
  waiting for transfers between devices  268 us (67%)
  matrix products  53.6 us (13%)
  local copies, waits for them, and re-layouts  46.8 us (12%)
  other arithmetic  13.3 us (3%)
  between operations  13.3 us (3%)
    all_gather x1, waiting for transfers between devices, body(): lax.all_gather(right_side, 'rows', axis=0, tiled=True)  80.9 us
    reduce_scatter x1, waiting for transfers between devices, body(): lax.psum_scatter(partial_in, 'rows', scatter_dimension=0, tiled=True)  70 us
    all_gather x1, waiting for transfers between devices, body(): lax.all_gather(left_next, 'cols', axis=1, tiled=True)  59.2 us
    reduce_scatter x1, waiting for transfers between devices, body(): lax.psum_scatter(partial_out, 'cols', scatter_dimension=1, tiled=True)  57.7 us
    dot_general x1, matrix products, body(): jnp.einsum('ikh,jkh->ijh', left_side, lax.all_gather(right_side, 'rows',...  31.6 us
    all_gather x1, local copies, waits for them, and re-layouts, body(): lax.all_gather(right_side, 'rows', axis=0, tiled=True)  21.7 us
    dot_general x1, matrix products, body(): jnp.einsum('kih,kjh->ijh', lax.all_gather(left_next, 'cols', axis=1, tile...  11.8 us
    transpose x1, local copies, waits for them, and re-layouts, body(): jnp.einsum('kih,kjh->ijh', lax.all_gather(left_next, 'cols', axis=1, tile...  9.8 us
  transfers between devices with their start and end apart: 4, of which 4 were waited for; matrix products, arithmetic and copies ran while one was open for 1% of the time, Pallas kernels for 0%

commit v1 on v0

v1 whole, which is shorter than its diff:
```python
import functools

import jax
import jax.numpy as jnp
from jax import lax
from jax.experimental import pallas as pl
from jax.experimental.pallas import tpu as pltpu
from jax.sharding import PartitionSpec as P

MESH = pl.DeviceIdType.MESH
eps = 1e-05
LANES = 128
SUB = 8
F32 = jnp.float32
BF16 = jnp.bfloat16


def high_low(values):
    high = values.astype(BF16)
    low = (values - high.astype(F32)).astype(BF16)
    return high, low


def columns_of(row):
    return jnp.broadcast_to(row, (LANES, LANES)).T


def block_transpose(parts, width):
    count, tiles = len(parts), len(parts[0])
    lane = lax.broadcasted_iota(jnp.int32, (SUB, LANES), 1)
    rolled = {}

    def turned(a, u, shift):
        key = (a, u, shift)
        if key not in rolled:
            rolled[key] = parts[a][u] if shift == 0 else pltpu.roll(parts[a][u], shift, 1)
        return rolled[key]

    out = []
    for b in range(count):
        row = []
        for t in range(tiles):
            acc = None
            at, end = t * LANES, (t + 1) * LANES
            while at < end:
                a = at // width
                source = b * width + at - a * width
                u = source // LANES
                stop = min(end, (a + 1) * width, at + (u + 1) * LANES - source)
                piece = turned(a, u, (at - source) % LANES)
                acc = piece if acc is None else jnp.where(lane >= at - t * LANES, piece, acc)
                at = stop
            row.append(acc)
        out.append(row)
    return out


def kernel(
    sizes,
    x_hbm,
    mask_hbm,
    norm_gain_hbm,
    norm_bias_hbm,
    proj_hbm,
    gate_hbm,
    out_gain_hbm,
    out_bias_hbm,
    out_hbm,
    y_ref,
    x_in,
    mask_in,
    norm_gain_in,
    norm_bias_in,
    proj_in,
    gate_in,
    out_gain_in,
    out_bias_in,
    out_in,
    weights,
    columns,
    mask_rows,
    mask_chunk,
    state,
    gating,
    normed,
    send_right,
    have_right,
    send_left,
    have_left,
    send_mixed,
    have_mixed,
    send_both,
    have_both,
    send_next,
    have_next,
    right_rows,
    right_cat,
    chunk_a,
    chunk_b,
    total,
    load_sem,
    send_sem,
    recv_sem,
):
    nr, nc, ri, cj = sizes
    slots = nr * nc
    rows_per = ri * cj // LANES
    chunks = ri // SUB
    per = rows_per // chunks
    tiles = nr * ri // LANES
    half = nr // SUB
    chunk_pos = per * LANES

    r, c = lax.axis_index("rows"), lax.axis_index("cols")
    me = c * nr + r
    pair, core = r // 2, lax.rem(r, 2)
    pairs = nr // 2
    cols = [lax.rem(c + d, nc) for d in range(nc)]
    cores = [core, 1 - core]
    order = [d for d in (4, 1, 7, 2, 6, 3, 5, 0) if d < nc]

    loads = [
        pltpu.make_async_copy(src, dst, load_sem.at[i])
        for i, (src, dst) in enumerate(
            (
                (x_hbm, x_in),
                (norm_gain_hbm, norm_gain_in),
                (norm_bias_hbm, norm_bias_in),
                (proj_hbm, proj_in),
                (mask_hbm, mask_in),
                (gate_hbm, gate_in),
                (out_gain_hbm, out_gain_in),
                (out_bias_hbm, out_bias_in),
                (out_hbm, out_in),
            )
        )
    ]
    for load in loads:
        load.start()

    def to_all(act):
        def step(i, carry):
            turned = []
            for d in range(pairs):
                far = lax.rem(i + d, pairs)
                turned.append((far, lax.rem(pair + far, pairs) * 2))
            for dx in order:
                for k in range(2):
                    far, base = turned[(dx + 4 * k) % pairs]
                    row = base + cores[k]

                    def go(row=row, dx=dx):
                        act(cols[dx] * nr + row, {"rows": row, "cols": cols[dx]})

                    if dx == 0 and k == 0:
                        pl.when(far != 0)(go)
                    else:
                        go()
            return carry

        lax.fori_loop(0, pairs, step, 0)

    barrier = pltpu.get_barrier_semaphore()
    to_all(lambda slot, device: pl.semaphore_signal(barrier, inc=1, device_id=device, device_id_type=MESH))

    def send(src, dst, stride, base, count, sem):
        def act(slot, device):
            pltpu.make_async_remote_copy(
                src_ref=src.at[pl.ds(slot * stride + base, count)],
                dst_ref=dst.at[pl.ds(me * stride + base, count)],
                send_sem=send_sem.at[sem],
                recv_sem=recv_sem.at[sem],
                device_id=device,
                device_id_type=MESH,
            ).start()

        to_all(act)
        for q in range(count):
            dst[pl.ds(me * stride + base + q, 1), :] = src[pl.ds(me * stride + base + q, 1), :]

    def await_bytes(buffer, count, sems, sem):
        span = buffer.at[pl.ds(0, (slots - 1) * count)]
        pltpu.make_async_copy(span, span, sems.at[sem]).wait()

    def prepare_weights(u):
        def one(values, at):
            high, low = high_low(values.T)
            rows = pl.ds(at * LANES, LANES)
            weights[u, rows, 0:LANES] = high
            weights[u, rows, LANES : 2 * LANES] = low
            weights[u, rows, 2 * LANES : 3 * LANES] = high

        for f in range(4):
            one(proj_in[u, :, f * LANES : (f + 1) * LANES], f)
        one(gate_in[u], 4)
        one(out_in[u], 5)

    def prepare_columns(u):
        for i, ref in enumerate((norm_gain_in, norm_bias_in, out_gain_in, out_bias_in)):
            columns[4 * u + i] = columns_of(ref[pl.ds(u, 1), :])

    def normalize(values, gain, bias):
        center = values - jnp.mean(values, axis=0, keepdims=True)
        spread = jnp.mean(center * center, axis=0, keepdims=True)
        return center * lax.rsqrt(spread + eps) * gain + bias

    def normalize_into(values, u, lanes, first):
        high, low = high_low(normalize(values, columns[4 * u + first], columns[4 * u + first + 1]))
        normed[0:LANES, lanes] = high
        normed[LANES : 2 * LANES, lanes] = high
        normed[2 * LANES : 3 * LANES, lanes] = low

    def product(u, first, count, lanes):
        return jnp.dot(
            weights[u, first * LANES : (first + count) * LANES, :],
            normed[:, lanes],
            preferred_element_type=F32,
        )

    def side(u, first, lanes, buffer, stride, base):
        hidden = product(u, first, 2, lanes)
        values = jax.nn.sigmoid(hidden[0:LANES]) * hidden[LANES:]
        for b in range(slots // SUB):
            for t in range(per):
                buffer[pl.ds(b * SUB * stride + base + t, SUB, stride=stride), :] = values[
                    b * SUB : (b + 1) * SUB, t * LANES : (t + 1) * LANES
                ]

    def chunk_lanes(k):
        return slice(k * chunk_pos, (k + 1) * chunk_pos)

    def gather_block(buffer, stride, base, b8):
        parts = [
            [
                buffer[pl.ds((a * nr + b8 * SUB) * stride + base + t, SUB, stride=stride), :]
                for t in range(per)
            ]
            for a in range(nc)
        ]
        return block_transpose(parts, cj)

    def scatter_block(parts, buffer, stride, base, b8):
        for a, row in enumerate(block_transpose(parts, cj)):
            for t in range(per):
                buffer[pl.ds((a * nr + b8 * SUB) * stride + base + t, SUB, stride=stride), :] = row[t]

    def finish(u, k, have):
        for t in range(per):
            q = k * per + t
            lanes = slice(q * LANES, (q + 1) * LANES)
            mixed = jnp.concatenate(
                [have[pl.ds(b * SUB * rows_per + q, SUB, stride=rows_per), :] for b in range(slots // SUB)], axis=0
            )
            normalize_into(mixed, u, lanes, 2)
        lanes = chunk_lanes(k)
        return state[:, lanes] + gating[:, lanes] * product(u, 5, 1, lanes)

    loads[0].wait()
    loads[1].wait()
    loads[2].wait()
    loads[3].wait()
    for load in loads[4:]:
        load.wait()
    prepare_weights(0)
    prepare_columns(0)
    for q in range(rows_per):
        lanes = slice(q * LANES, (q + 1) * LANES)
        values = x_in[q * LANES : (q + 1) * LANES, :].T
        state[:, lanes] = values
        normalize_into(values, 0, lanes, 0)
    for k in range(chunks):
        side(0, 2, chunk_lanes(k), send_right, rows_per, k * per)
    pl.semaphore_wait(barrier, slots - 1)
    send(send_right, have_right, rows_per, 0, rows_per, 0)
    for k in range(chunks):
        side(0, 0, chunk_lanes(k), send_left, rows_per, k * per)
        send(send_left, have_left, rows_per, k * per, per, 1 + k)
    for k in range(chunks):
        gating[:, chunk_lanes(k)] = jax.nn.sigmoid(product(0, 4, 1, chunk_lanes(k)))
    prepare_weights(1)
    prepare_columns(1)
    mask = mask_in[...].astype(F32)
    for t in range(tiles):
        mask_rows[t * LANES : (t + 1) * LANES, :] = columns_of(mask[t : t + 1, :])
    for k in range(chunks):
        for b in range(SUB):
            for b8 in range(half):
                mask_chunk[k, pl.ds(b * nr + b8 * SUB, SUB), :] = mask_rows[
                    pl.ds(b8 * SUB * ri + k * SUB + b, SUB, stride=ri), :
                ]

    await_bytes(have_right, rows_per, recv_sem, 0)
    for k in range(chunks):
        for b8 in range(half):
            for b, row in enumerate(gather_block(have_right, rows_per, k * per, b8)):
                for t in range(tiles):
                    right_rows[pl.ds(t * nr * ri + b8 * SUB * ri + k * SUB + b, SUB, stride=ri), :] = row[t]
    tokens = nr * ri
    for t in range(tiles):
        high, low = high_low(right_rows[t * tokens : (t + 1) * tokens, :] * mask_rows[...])
        right_cat[:, t * LANES : (t + 1) * LANES] = high
        right_cat[:, tokens + t * LANES : tokens + (t + 1) * LANES] = high
        right_cat[:, 2 * tokens + t * LANES : 2 * tokens + (t + 1) * LANES] = low
    for k in range(chunks):
        await_bytes(have_left, per, recv_sem, 1 + k)
        for b8 in range(half):
            for b, row in enumerate(gather_block(have_left, rows_per, k * per, b8)):
                for t in range(tiles):
                    chunk_a[pl.ds(b * nr + b8 * SUB, SUB), t * LANES : (t + 1) * LANES] = (
                        row[t] * mask[t : t + 1, :] * mask_chunk[k, pl.ds(b * nr + b8 * SUB, SUB), :]
                    )
        high, low = high_low(chunk_a[...])
        chunk_b[...] = lax.dot_general(
            jnp.concatenate([high, low, high], axis=1),
            right_cat[...],
            (((1,), (1,)), ((), ())),
            preferred_element_type=F32,
        )
        for b8 in range(half):
            parts = [
                [chunk_b[pl.ds(b * nr + b8 * SUB, SUB), t * LANES : (t + 1) * LANES] for t in range(tiles)]
                for b in range(SUB)
            ]
            scatter_block(parts, send_mixed, rows_per, k * per, b8)
        send(send_mixed, have_mixed, rows_per, k * per, per, 4 + k)

    for k in range(chunks):
        await_bytes(have_mixed, per, recv_sem, 4 + k)
        lanes = chunk_lanes(k)
        state[:, lanes] = finish(0, k, have_mixed)
        for t in range(per):
            q = k * per + t
            tile = slice(q * LANES, (q + 1) * LANES)
            normalize_into(state[:, tile], 1, tile, 0)
        side(1, 0, lanes, send_both, 2 * rows_per, 2 * per * k)
        side(1, 2, lanes, send_both, 2 * rows_per, 2 * per * k + per)
        send(send_both, have_both, 2 * rows_per, 2 * per * k, 2 * per, 7 + k)
        gating[:, lanes] = jax.nn.sigmoid(product(1, 4, 1, lanes))

    for k in range(chunks):
        await_bytes(have_both, 2 * per, recv_sem, 7 + k)
        for b8 in range(half):
            for b, row in enumerate(gather_block(have_both, 2 * rows_per, 2 * per * k, b8)):
                for t in range(tiles):
                    chunk_a[pl.ds(b * nr + b8 * SUB, SUB), t * LANES : (t + 1) * LANES] = row[t] * mask[t : t + 1, :]
            for b, row in enumerate(gather_block(have_both, 2 * rows_per, 2 * per * k + per, b8)):
                for t in range(tiles):
                    chunk_b[pl.ds(b * nr + b8 * SUB, SUB), t * LANES : (t + 1) * LANES] = (
                        row[t] * mask[t : t + 1, :] * mask_chunk[k, pl.ds(b * nr + b8 * SUB, SUB), :]
                    )
        left_t = jnp.concatenate(
            [chunk_a[:, t * LANES : (t + 1) * LANES].T for t in range(tiles)], axis=0
        )
        high, low = high_low(left_t)
        right_high, right_low = high_low(chunk_b[...])
        part = jnp.dot(
            jnp.concatenate([high, low, high], axis=1),
            jnp.concatenate([right_high, right_high, right_low], axis=0),
            preferred_element_type=F32,
        )
        for t in range(tiles):
            rows = slice(t * tokens, (t + 1) * tokens)
            if k == 0:
                total[rows, :] = part[:, t * LANES : (t + 1) * LANES]
            else:
                total[rows, :] += part[:, t * LANES : (t + 1) * LANES]
    for k in range(chunks):
        for b8 in range(half):
            parts = [
                [
                    total[pl.ds(t * tokens + b8 * SUB * ri + k * SUB + b, SUB, stride=ri), :]
                    for t in range(tiles)
                ]
                for b in range(SUB)
            ]
            scatter_block(parts, send_next, rows_per, k * per, b8)
        send(send_next, have_next, rows_per, k * per, per, 10 + k)
    for k in range(chunks):
        await_bytes(have_next, per, recv_sem, 10 + k)
        values = finish(1, k, have_next)
        for t in range(per):
            q = k * per + t
            y_ref[q * LANES : (q + 1) * LANES, :] = values[:, t * LANES : (t + 1) * LANES].T

    await_bytes(send_right, rows_per, send_sem, 0)
    for k in range(chunks):
        await_bytes(send_left, per, send_sem, 1 + k)
        await_bytes(send_mixed, per, send_sem, 4 + k)
        await_bytes(send_both, 2 * per, send_sem, 7 + k)
        await_bytes(send_next, per, send_sem, 10 + k)


def body(
    nr,
    nc,
    pair_state,
    token_mask,
    norm_gain,
    norm_bias,
    proj_weight,
    gate_weight,
    out_gain,
    out_bias,
    out_weight,
):
    ri, cj, channels = pair_state.shape
    hidden = proj_weight.shape[2] // 4
    tokens = token_mask.shape[0]
    slots = nr * nc
    positions = ri * cj
    assert slots == hidden == channels == LANES
    assert nr % SUB == 0 and ri % SUB == 0 and tokens == nr * ri == nc * cj and tokens % LANES == 0
    assert nc == SUB and SUB * cj == tokens and positions % LANES == 0
    rows_per = positions // LANES
    chunks = ri // SUB
    message = pltpu.VMEM((slots * rows_per, LANES), F32)
    double = pltpu.VMEM((slots * 2 * rows_per, LANES), F32)
    inputs = (
        pair_state.reshape(positions, channels),
        token_mask.reshape(tokens // LANES, LANES),
        norm_gain,
        norm_bias,
        proj_weight,
        gate_weight,
        out_gain,
        out_bias,
        out_weight,
    )
    result = pl.pallas_call(
        functools.partial(kernel, (nr, nc, ri, cj)),
        out_shape=jax.ShapeDtypeStruct((positions, channels), F32),
        in_specs=[pl.BlockSpec(memory_space=pl.ANY)] * len(inputs),
        out_specs=pl.BlockSpec(memory_space=pltpu.VMEM),
        scratch_shapes=[
            *(pltpu.VMEM(i.shape, i.dtype) for i in inputs),
            pltpu.VMEM((2, 6 * LANES, 3 * LANES), BF16),
            pltpu.VMEM((8, LANES, LANES), F32),
            pltpu.VMEM((tokens, LANES), F32),
            pltpu.VMEM((chunks, SUB * nr, LANES), F32),
            pltpu.VMEM((channels, positions), F32),
            pltpu.VMEM((channels, positions), F32),
            pltpu.VMEM((3 * LANES, positions), BF16),
            message,
            message,
            message,
            message,
            message,
            message,
            double,
            double,
            message,
            message,
            pltpu.VMEM((tokens // LANES * tokens, LANES), F32),
            pltpu.VMEM((tokens, 3 * tokens), BF16),
            pltpu.VMEM((SUB * nr, tokens), F32),
            pltpu.VMEM((SUB * nr, tokens), F32),
            pltpu.VMEM((tokens // LANES * tokens, LANES), F32),
            pltpu.SemaphoreType.DMA((len(inputs),)),
            pltpu.SemaphoreType.DMA((1 + 4 * chunks,)),
            pltpu.SemaphoreType.DMA((1 + 4 * chunks,)),
        ],
        compiler_params=pltpu.CompilerParams(
            collective_id=0, has_side_effects=True, vmem_limit_bytes=48 * 2**20
        ),
        name="triangles",
    )(*inputs)
    return result.reshape(pair_state.shape)


def solution(mesh):
    placed = (P(("groups", "rows"), "cols", None), P("groups"), P(), P(), P(), P(), P(), P(), P())
    return jax.shard_map(
        functools.partial(body, mesh.shape["rows"], mesh.shape["cols"]),
        mesh=mesh,
        in_specs=placed,
        out_specs=P(("groups", "rows"), "cols", None),
        check_vma=False,
    )
```

time: 398 us -> 121 us (0.30)
  waiting for transfers between devices: 268 us -> 0 us
  Pallas kernels: 0 us -> 114 us
  matrix products: 53.6 us -> 0 us
  local copies, waits for them, and re-layouts: 46.8 us -> 7.46 us
  other arithmetic: 13.3 us -> 0 us
  between operations: 13.3 us -> 0.02 us
    all_gather x2 -> x0, waiting for transfers between devices: 140 us -> none  [the longest x1 80.9 us: body(): lax.all_gather(right_side, 'rows', axis=0, tiled=True)]
    reduce_scatter x2 -> x0, waiting for transfers between devices: 128 us -> none  [the longest x1 70 us: body(): lax.psum_scatter(partial_in, 'rows', scatter_dimension=0, tiled=True)]
    pallas_call x0 -> x1, Pallas kernels: none -> 114 us  [body(): pl.pallas_call(functools.partial(kernel, (nr, nc, ri, cj)), out_shape=jax...]
    dot_general x8 -> x0, matrix products: 53.6 us -> none  [the longest x1 31.6 us: body(): jnp.einsum('ikh,jkh->ijh', left_side, lax.all_gather(right_side, 'rows',...]
    all_gather x2 -> x0, local copies, waits for them, and re-layouts: 27.9 us -> none  [the longest x1 21.7 us: body(): lax.all_gather(right_side, 'rows', axis=0, tiled=True)]
    transpose x2 -> x0, local copies, waits for them, and re-layouts: 15.8 us -> none  [the longest x1 9.8 us: body(): jnp.einsum('kih,kjh->ijh', lax.all_gather(left_next, 'cols', axis=1, tile...]
    reduce_sum x7 -> x0, other arithmetic: 8.71 us -> none  [the longest x4 4.85 us: normalize(): spread = jnp.mean(center * center, axis=-1, keepdims=True)]
    unnamed x12 -> x19, local copies, waits for them, and re-layouts: 0.77 us -> 7.46 us
  transfers between devices with their start and end apart: 4 -> 0, of which waited for: 4 -> 0; matrix products, arithmetic and copies ran while one was open for 1% -> 0% of each run, Pallas kernels for 0% -> 0%
where the time goes in v1:
time: 121 us
  Pallas kernels  114 us (94%)
  local copies, waits for them, and re-layouts  7.46 us (6%)
    pallas_call x1, Pallas kernels, body(): pl.pallas_call(functools.partial(kernel, (nr, nc, ri, cj)), out_shape=jax...  114 us
    unnamed x19, local copies, waits for them, and re-layouts  7.46 us

profile of v1, /device:TPU:513, one launch (start us, length us, event | category | flops | bytes accessed | tf_op | source)
XLA Modules:
  0.0 121.1 jit_solution(1646297095382005084)
XLA Ops:
  0.0 0.0 copy-start.4
  0.0 0.0 copy-start.5
  0.0 0.7 copy-done.4
  0.7 0.0 copy-done.5
  0.7 0.0 copy-start
  0.7 1.1 copy-done
  1.8 0.0 copy-start.1
  1.8 1.0 copy-done.1
  2.8 0.0 copy-start.2
  2.8 0.9 copy-done.2
  3.7 0.0 copy-start.3
  3.7 0.9 copy-done.3
  4.6 0.0 copy-start.6
  4.6 0.7 copy-done.6
  5.3 0.0 copy-start.7
  5.3 0.7 copy-done.7
  6.0 0.0 copy-start.8
  6.0 0.7 copy-done.8
  6.7 113.6 %triangles.1 = f32[1152,128]{1,0:T(8,128)S(1)} custom-call(f32[1152,128]{1,0:T(8,128)S(1)} %bitcast.4, s32[3,128]{1,0:T(4,128)S(1)} %bitcast.5, f32[2,128]{1,0:T(2,128)S(1)} %copy-done.5, f32[2,128]{1,0:T(2,128)S(1)} %copy-done.6, f32[2,128,512]{2,1,0:T(8,128)S(1)} %copy-done.1, f32[2,128,128]{2,1,0:T(8,128)S(1)} %copy-done.2, f32[2,128]{1,0:T(2,128)S(1)} %copy-done.7, ...), custom_call_target="tpu_custom_call" | custom-call | tf_op jit(solution)/shard_map/triangles/pallas_call | solution.py:429
  120.3 0.8 copy.11
Async XLA Ops:
  0.0 0.7 copy-start.4
  0.0 0.7 copy-start.5
  0.7 1.1 copy-start
  1.8 1.0 copy-start.1
  2.8 0.9 copy-start.2
  3.7 0.9 copy-start.3
  4.6 0.7 copy-start.6
  5.3 0.7 copy-start.7
  6.0 0.7 copy-start.8

commit v2 on v1

v2 whole, which is shorter than its diff:
```python
import functools

import jax
import jax.numpy as jnp
from jax import lax
from jax.experimental import pallas as pl
from jax.experimental.pallas import tpu as pltpu
from jax.sharding import PartitionSpec as P

MESH = pl.DeviceIdType.MESH
eps = 1e-05
LANES = 128
SUB = 8
F32 = jnp.float32
BF16 = jnp.bfloat16


def high_low(values):
    high = values.astype(BF16)
    low = (values - high.astype(F32)).astype(BF16)
    return high, low


def columns_of(row):
    return jnp.broadcast_to(row, (LANES, LANES)).T


def swap_blocks(parts):
    width = LANES // SUB
    block = lax.broadcasted_iota(jnp.int32, (SUB, LANES), 1) // width
    parts = list(parts)
    for step in (1, 2, 4):
        odd = (block // step) % 2 == 1
        for a in range(SUB):
            if (a // step) % 2 == 0:
                low, high = parts[a], parts[a + step]
                parts[a] = jnp.where(odd, pltpu.roll(high, step * width, 1), low)
                parts[a + step] = jnp.where(odd, high, pltpu.roll(low, LANES - step * width, 1))
    return parts


def kernel(
    sizes,
    x_hbm,
    mask_hbm,
    norm_gain_hbm,
    norm_bias_hbm,
    proj_hbm,
    gate_hbm,
    out_gain_hbm,
    out_bias_hbm,
    out_hbm,
    y_ref,
    x_in,
    mask_in,
    norm_gain_in,
    norm_bias_in,
    proj_in,
    gate_in,
    out_gain_in,
    out_bias_in,
    out_in,
    weights,
    columns,
    mask_rows,
    mask_lanes,
    mask_near,
    mask_far,
    state,
    gating,
    normed,
    send_first,
    have_first,
    send_mixed,
    have_mixed,
    send_second,
    have_second,
    send_next,
    have_next,
    rows_a,
    rows_b,
    left_cat,
    right_cat,
    under_cat,
    blocks,
    load_sem,
    send_sem,
    recv_sem,
):
    nr, nc, ri, cj = sizes
    slots = nr * nc
    groups = ri // SUB
    half = nr // SUB
    tokens = nr * ri
    span = SUB * nr
    last = groups - 1
    early = [(a, b) for a in range(last) for b in range(last)]
    order = early + [(last, b) for b in range(last)] + [(a, last) for a in range(groups)]
    count = len(order)
    cut_a, cut_b = len(early), len(early) + last
    place = {ab: p for p, ab in enumerate(order)}

    r, c = lax.axis_index("rows"), lax.axis_index("cols")
    me = c * nr + r
    pair, core = r // 2, lax.rem(r, 2)
    pairs = nr // 2
    cols = [lax.rem(c + d, nc) for d in range(nc)]
    cores = [core, 1 - core]
    rows_at = [lax.rem(pair + d, pairs) * 2 for d in range(pairs)]
    turns = [d for d in (4, 1, 7, 2, 6, 3, 5, 0) if d < nc]

    loads = [
        pltpu.make_async_copy(src, dst, load_sem.at[i])
        for i, (src, dst) in enumerate(
            (
                (x_hbm, x_in),
                (norm_gain_hbm, norm_gain_in),
                (norm_bias_hbm, norm_bias_in),
                (proj_hbm, proj_in),
                (mask_hbm, mask_in),
                (gate_hbm, gate_in),
                (out_gain_hbm, out_gain_in),
                (out_bias_hbm, out_bias_in),
                (out_hbm, out_in),
            )
        )
    ]
    for load in loads:
        load.start()

    def to_all(act):
        def step(i, carry):
            turn, odd = i // 2, lax.rem(i, 2)
            away = pairs // 2 + turn - odd * (2 * turn + 1)
            far_row = lax.rem(pair + away, pairs) * 2
            far_col = lax.rem(c + away, nc)
            for d in turns:
                for k in range(2):
                    row, col = (far_row + cores[0], cols[d]) if k == 0 else (rows_at[d] + cores[1], far_col)

                    def go(row=row, col=col):
                        act(col * nr + row, {"rows": row, "cols": col})

                    if d == 0 and k == 0:
                        pl.when(away != 0)(go)
                    else:
                        go()
            return carry

        lax.fori_loop(0, pairs, step, 0)

    barrier = pltpu.get_barrier_semaphore()
    to_all(lambda slot, device: pl.semaphore_signal(barrier, inc=1, device_id=device, device_id_type=MESH))

    def send(src, dst, stride, base, rows, sem):
        def act(slot, device):
            pltpu.make_async_remote_copy(
                src_ref=src.at[pl.ds(slot * stride + base, rows)],
                dst_ref=dst.at[pl.ds(me * stride + base, rows)],
                send_sem=send_sem.at[sem],
                recv_sem=recv_sem.at[sem],
                device_id=device,
                device_id_type=MESH,
            ).start()

        to_all(act)
        for q in range(rows):
            dst[pl.ds(me * stride + base + q, 1), :] = src[pl.ds(me * stride + base + q, 1), :]

    def await_bytes(buffer, rows, sems, sem):
        whole = buffer.at[pl.ds(0, (slots - 1) * rows)]
        pltpu.make_async_copy(whole, whole, sems.at[sem]).wait()

    def prepare_weights(u):
        def one(values, at):
            high, low = high_low(values.T)
            rows = pl.ds(at * LANES, LANES)
            weights[u, rows, 0:LANES] = high
            weights[u, rows, LANES : 2 * LANES] = low
            weights[u, rows, 2 * LANES : 3 * LANES] = high

        for f in range(4):
            one(proj_in[u, :, f * LANES : (f + 1) * LANES], f)
        one(gate_in[u], 4)
        one(out_in[u], 5)

    def prepare_columns(u):
        for i, ref in enumerate((norm_gain_in, norm_bias_in, out_gain_in, out_bias_in)):
            columns[4 * u + i] = columns_of(ref[pl.ds(u, 1), :])

    def lanes_of(first, number=1):
        return slice(first * LANES, (first + number) * LANES)

    def normalize(values, gain, bias):
        center = values - jnp.mean(values, axis=0, keepdims=True)
        spread = jnp.mean(center * center, axis=0, keepdims=True)
        return center * lax.rsqrt(spread + eps) * gain + bias

    def normalize_into(values, u, at, first):
        high, low = high_low(normalize(values, columns[4 * u + first], columns[4 * u + first + 1]))
        normed[0:LANES, lanes_of(at)] = high
        normed[LANES : 2 * LANES, lanes_of(at)] = high
        normed[2 * LANES : 3 * LANES, lanes_of(at)] = low

    def product(u, first, number, at, tiles):
        return jnp.dot(
            weights[u, first * LANES : (first + number) * LANES, :],
            normed[:, lanes_of(at, tiles)],
            preferred_element_type=F32,
        )

    def side(u, first, at, tiles, buffer, stride, base):
        hidden = product(u, first, 2, at, tiles)
        values = jax.nn.sigmoid(hidden[0:LANES]) * hidden[LANES:]
        for b in range(slots // SUB):
            for t in range(tiles):
                buffer[pl.ds(b * SUB * stride + base + t, SUB, stride=stride), :] = values[
                    b * SUB : (b + 1) * SUB, lanes_of(t)
                ]

    def at_owner(buffer, stride, row, b8):
        return swap_blocks(
            [buffer[pl.ds((a * nr + b8 * SUB) * stride + row, SUB, stride=stride), :] for a in range(nc)]
        )

    def to_owners(parts, buffer, stride, row, b8):
        for a, part in enumerate(swap_blocks(parts)):
            buffer[pl.ds((a * nr + b8 * SUB) * stride + row, SUB, stride=stride), :] = part

    def finish(u, first, number, have):
        for t in range(number):
            normalize_into(
                jnp.concatenate(
                    [have[pl.ds(b * SUB * count + first + t, SUB, stride=count), :] for b in range(slots // SUB)],
                    axis=0,
                ),
                u,
                t,
                2,
            )
        lanes = lanes_of(first, number)
        return state[:, lanes] + gating[:, lanes] * product(u, 5, 1, 0, number)

    def pieces(p):
        a, b = order[p]
        return [
            slice(at, at + SUB)
            for t in range(SUB)
            for parity in range(2)
            for at in ((a * SUB + t) * cj + parity * ri + b * SUB,)
        ]

    for load in loads:
        load.wait()
    prepare_weights(0)
    prepare_columns(0)
    for a in range(groups):
        for b in range(groups):
            p = place[a, b]
            values = jnp.concatenate([x_in[rows, :] for rows in pieces(p)], axis=0).T
            state[:, lanes_of(p)] = values
            normalize_into(values, 0, a * groups + b, 0)
        side(0, 0, a * groups, groups, send_first, 2 * count, 2 * groups * a)
        side(0, 2, a * groups, groups, send_first, 2 * count, 2 * groups * a + groups)
        if a == 0:
            with jax.named_scope("barrier"):
                pl.semaphore_wait(barrier, slots - 1)
        with jax.named_scope("send_first"):
            send(send_first, have_first, 2 * count, 2 * groups * a, 2 * groups, a)
    for a in range(groups):
        gate = jax.nn.sigmoid(product(0, 4, 1, a * groups, groups))
        for b in range(groups):
            gating[:, lanes_of(place[a, b])] = gate[:, lanes_of(b)]
    prepare_weights(1)
    prepare_columns(1)
    mask = mask_in[...].astype(F32)
    for t in range(tokens // LANES):
        mask_rows[lanes_of(t), :] = columns_of(mask[t : t + 1, :])
    for a in range(groups):
        near = jnp.concatenate(
            [mask_rows[q * ri + a * SUB : q * ri + (a + 1) * SUB, :] for q in range(nr)], axis=0
        )
        mask_near[lanes_of(a), :] = near
        mask_lanes[a] = near.T[0:SUB, :]
        for t in range(SUB):
            for b8 in range(half):
                mask_far[pl.ds(a * span + t * nr + b8 * SUB, SUB), :] = mask_rows[
                    pl.ds(b8 * SUB * ri + a * SUB + t, SUB, stride=ri), :
                ]

    def send_blocks(first, number, buffer, have, sem, strided):
        for p in range(first, first + number):
            for b8 in range(half):
                if strided:
                    parts = [blocks[pl.ds(p * span + b8 * SUB * SUB + t, SUB, stride=SUB), :] for t in range(SUB)]
                else:
                    parts = [blocks[pl.ds(p * span + t * nr + b8 * SUB, SUB), :] for t in range(SUB)]
                to_owners(parts, buffer, count, p, b8)
        send(buffer, have, count, first, number, sem)

    def keep_blocks(values, firsts, seconds):
        for i, a in enumerate(firsts):
            for j, b in enumerate(seconds):
                blocks[lanes_of(place[a, b]), :] = values[i * span : (i + 1) * span, lanes_of(j)]

    near_groups = list(range(last))
    all_groups = list(range(groups))

    def far_times_near(firsts, seconds):
        values = lax.dot_general(
            left_cat[firsts[0] * span : (firsts[-1] + 1) * span, :],
            right_cat[seconds[0] * span : (seconds[-1] + 1) * span, :],
            (((1,), (1,)), ((), ())),
            preferred_element_type=F32,
        )
        keep_blocks(values, firsts, seconds)

    for a in range(groups):
        with jax.named_scope("wait_first"):
            await_bytes(have_first, 2 * groups, recv_sem, a)
        for b in range(groups):
            for b8 in range(half):
                for t, part in enumerate(at_owner(have_first, 2 * count, 2 * groups * a + b, b8)):
                    rows_a[pl.ds(b * span + t * nr + b8 * SUB, SUB), :] = part
                for t, part in enumerate(at_owner(have_first, 2 * count, 2 * groups * a + groups + b, b8)):
                    rows_b[pl.ds(b * span + b8 * SUB * SUB + t, SUB, stride=SUB), :] = part
        for b in range(groups):
            high, low = high_low(
                rows_a[lanes_of(b), :] * mask_lanes[b, 0:1, :] * mask_far[a * span : (a + 1) * span, :]
            )
            rows = slice(a * span, (a + 1) * span)
            left_cat[rows, lanes_of(b)] = high
            left_cat[rows, lanes_of(groups + b)] = low
            left_cat[rows, lanes_of(2 * groups + b)] = high
            high, low = high_low(rows_b[lanes_of(b), :] * mask_near[lanes_of(a), :])
            right_cat[rows, lanes_of(b)] = high
            right_cat[rows, lanes_of(groups + b)] = high
            right_cat[rows, lanes_of(2 * groups + b)] = low
        if a == last - 1:
            far_times_near(near_groups, near_groups)
            with jax.named_scope("send_mixed"):
                send_blocks(0, cut_a, send_mixed, have_mixed, groups, False)
    far_times_near([last], near_groups)
    far_times_near(all_groups, [last])
    with jax.named_scope("send_mixed"):
        send_blocks(cut_a, count - cut_a, send_mixed, have_mixed, groups + 1, False)

    def project_second(first, number, sem):
        side(1, 0, 0, number, send_second, 2 * count, 2 * first)
        side(1, 2, 0, number, send_second, 2 * count, 2 * first + number)
        with jax.named_scope("send_second"):
            send(send_second, have_second, 2 * count, 2 * first, 2 * number, sem)
        gating[:, lanes_of(first, number)] = jax.nn.sigmoid(product(1, 4, 1, 0, number))

    second_sets = ((0, cut_a), (cut_a, cut_b), (cut_b, count))
    for i, (first, stop) in enumerate(second_sets):
        number = stop - first
        if i < 2:
            with jax.named_scope("wait_mixed"):
                await_bytes(have_mixed, (cut_a, count - cut_a)[i], recv_sem, groups + i)
        values = finish(0, first, number, have_mixed)
        state[:, lanes_of(first, number)] = values
        for t in range(number):
            normalize_into(state[:, lanes_of(first + t)], 1, t, 0)
        project_second(first, number, groups + 2 + i)

    def under_times(firsts, seconds):
        values = jnp.dot(
            left_cat[firsts[0] * span : (firsts[-1] + 1) * span, :],
            under_cat[:, seconds[0] * span : (seconds[-1] + 1) * span],
            preferred_element_type=F32,
        )
        keep_blocks(values, firsts, seconds)

    for i, (first, stop) in enumerate(second_sets):
        number = stop - first
        with jax.named_scope("wait_second"):
            await_bytes(have_second, 2 * number, recv_sem, groups + 2 + i)
        for p in range(first, stop):
            a, b = order[p]
            row = first + p
            for b8 in range(half):
                for t, part in enumerate(at_owner(have_second, 2 * count, row, b8)):
                    rows_a[pl.ds(t * nr + b8 * SUB, SUB), :] = part
                for t, part in enumerate(at_owner(have_second, 2 * count, row + number, b8)):
                    rows_b[pl.ds(t * nr + b8 * SUB, SUB), :] = part
            high, low = high_low((rows_a[0:span, :] * mask_lanes[b, 0:1, :]).T)
            rows = slice(b * span, (b + 1) * span)
            left_cat[rows, lanes_of(a)] = high
            left_cat[rows, lanes_of(groups + a)] = low
            left_cat[rows, lanes_of(2 * groups + a)] = high
            high, low = high_low(
                rows_b[0:span, :] * mask_lanes[b, 0:1, :] * mask_far[a * span : (a + 1) * span, :]
            )
            under_cat[lanes_of(a), lanes_of(b)] = high
            under_cat[lanes_of(groups + a), lanes_of(b)] = high
            under_cat[lanes_of(2 * groups + a), lanes_of(b)] = low
        if i == 1:
            under_times(near_groups, near_groups)
            with jax.named_scope("send_next"):
                send_blocks(0, cut_a, send_next, have_next, groups + 5, True)
    under_times([last], near_groups)
    under_times(all_groups, [last])
    with jax.named_scope("send_next"):
        send_blocks(cut_a, count - cut_a, send_next, have_next, groups + 6, True)
    for i, (first, stop) in enumerate(((0, cut_a), (cut_a, count))):
        with jax.named_scope("wait_next"):
            await_bytes(have_next, stop - first, recv_sem, groups + 5 + i)
        values = finish(1, first, stop - first, have_next)
        for p in range(first, stop):
            tile = values[:, lanes_of(p - first)].T
            for q, rows in enumerate(pieces(p)):
                y_ref[rows, :] = tile[q * SUB : (q + 1) * SUB, :]

    for a in range(groups):
        await_bytes(send_first, 2 * groups, send_sem, a)
    for i, rows in enumerate((cut_a, count - cut_a)):
        await_bytes(send_mixed, rows, send_sem, groups + i)
        await_bytes(send_next, rows, send_sem, groups + 5 + i)
    for i, (first, stop) in enumerate(second_sets):
        await_bytes(send_second, 2 * (stop - first), send_sem, groups + 2 + i)


def body(
    nr,
    nc,
    pair_state,
    token_mask,
    norm_gain,
    norm_bias,
    proj_weight,
    gate_weight,
    out_gain,
    out_bias,
    out_weight,
):
    ri, cj, channels = pair_state.shape
    hidden = proj_weight.shape[2] // 4
    tokens = token_mask.shape[0]
    slots = nr * nc
    positions = ri * cj
    assert slots == hidden == channels == LANES
    assert nc == SUB and nr == 2 * nc and cj == 2 * ri and tokens == nr * ri == nc * cj
    assert ri % SUB == 0 and ri > SUB and tokens % LANES == 0
    groups = ri // SUB
    count = groups * groups
    message = pltpu.VMEM((slots * count, LANES), F32)
    double = pltpu.VMEM((slots * 2 * count, LANES), F32)
    inputs = (
        pair_state.reshape(positions, channels),
        token_mask.reshape(tokens // LANES, LANES),
        norm_gain,
        norm_bias,
        proj_weight,
        gate_weight,
        out_gain,
        out_bias,
        out_weight,
    )
    result = pl.pallas_call(
        functools.partial(kernel, (nr, nc, ri, cj)),
        out_shape=jax.ShapeDtypeStruct((positions, channels), F32),
        in_specs=[pl.BlockSpec(memory_space=pltpu.HBM)] * len(inputs),
        out_specs=pl.BlockSpec(memory_space=pltpu.VMEM),
        scratch_shapes=[
            *(pltpu.VMEM(i.shape, i.dtype) for i in inputs),
            pltpu.VMEM((2, 6 * LANES, 3 * LANES), BF16),
            pltpu.VMEM((8, LANES, LANES), F32),
            pltpu.VMEM((tokens, LANES), F32),
            pltpu.VMEM((groups, SUB, LANES), F32),
            pltpu.VMEM((tokens, LANES), F32),
            pltpu.VMEM((tokens, LANES), F32),
            pltpu.VMEM((channels, positions), F32),
            pltpu.VMEM((channels, positions), F32),
            pltpu.VMEM((3 * LANES, positions), BF16),
            double,
            double,
            message,
            message,
            double,
            double,
            message,
            message,
            pltpu.VMEM((tokens, LANES), F32),
            pltpu.VMEM((tokens, LANES), F32),
            pltpu.VMEM((tokens, 3 * tokens), BF16),
            pltpu.VMEM((tokens, 3 * tokens), BF16),
            pltpu.VMEM((3 * tokens, tokens), BF16),
            pltpu.VMEM((count * LANES, LANES), F32),
            pltpu.SemaphoreType.DMA((len(inputs),)),
            pltpu.SemaphoreType.DMA((groups + 7,)),
            pltpu.SemaphoreType.DMA((groups + 7,)),
        ],
        compiler_params=pltpu.CompilerParams(
            collective_id=0, has_side_effects=True, vmem_limit_bytes=48 * 2**20
        ),
        name="triangles",
    )(*(pltpu.with_memory_space_constraint(i, pltpu.HBM) for i in inputs))
    return result.reshape(pair_state.shape)


def solution(mesh):
    placed = (P(("groups", "rows"), "cols", None), P("groups"), P(), P(), P(), P(), P(), P(), P())
    return jax.shard_map(
        functools.partial(body, mesh.shape["rows"], mesh.shape["cols"]),
        mesh=mesh,
        in_specs=placed,
        out_specs=P(("groups", "rows"), "cols", None),
        check_vma=False,
    )
```

time: 121 us -> 109 us (0.901)
  local copies, waits for them, and re-layouts: 7.46 us -> 0.82 us
  Pallas kernels: 114 us -> 108 us
    unnamed x19 -> x1, local copies, waits for them, and re-layouts: 7.46 us -> 0.82 us
    pallas_call x1, Pallas kernels: 114 us -> 108 us  [body(): pl.pallas_call(functools.partial(kernel, (nr, nc, ri, cj)), out_shape=jax...]
where the time goes in v2:
time: 109 us
  Pallas kernels  108 us (99%)
    pallas_call x1, Pallas kernels, body(): pl.pallas_call(functools.partial(kernel, (nr, nc, ri, cj)), out_shape=jax...  108 us

profile of v2, /device:TPU:513, one launch (start us, length us, event | category | flops | bytes accessed | tf_op | source)
XLA Modules:
  0.0 108.9 jit_solution(9557996428575200705)
XLA Ops:
  0.0 108.0 %triangles.1 = f32[1152,128]{1,0:T(8,128)S(1)} custom-call(f32[1152,128]{1,0:T(8,128)} %bitcast.4, s32[3,128]{1,0:T(4,128)} %bitcast.5, f32[2,128]{1,0:T(2,128)} %norm_gain_hbm.1, f32[2,128]{1,0:T(2,128)} %norm_bias_hbm.1, f32[2,128,512]{2,1,0:T(8,128)} %proj_hbm.1, f32[2,128,128]{2,1,0:T(8,128)} %gate_hbm.1, f32[2,128]{1,0:T(2,128)} %out_gain_hbm.1, ...), custom_call_target="tpu_custom_call" | custom-call | tf_op jit(solution)/shard_map/triangles/pallas_call | solution.py:460
  108.0 0.8 copy.11

commit v3 on v2

--- a/solution.py
+++ b/solution.py
@@ -128,8 +128,27 @@
     for load in loads:
         load.start()
 
-    def to_all(act):
-        def step(i, carry):
+    def to_all(act, how):
+        def mixed(i, carry):
+            turned = []
+            for d in range(pairs):
+                far = lax.rem(i + d, pairs)
+                turned.append((far, lax.rem(pair + far, pairs) * 2))
+            for dx in turns:
+                for k in range(2):
+                    far, base = turned[(dx + 4 * k) % pairs]
+                    row = base + cores[k]
+
+                    def go(row=row, dx=dx):
+                        act(cols[dx] * nr + row, {"rows": row, "cols": cols[dx]})
+
+                    if dx == 0 and k == 0:
+                        pl.when(far != 0)(go)
+                    else:
+                        go()
+            return carry
+
+        def far_first(i, carry):
             turn, odd = i // 2, lax.rem(i, 2)
             away = pairs // 2 + turn - odd * (2 * turn + 1)
             far_row = lax.rem(pair + away, pairs) * 2
@@ -147,12 +166,26 @@
                         go()
             return carry
 
-        lax.fori_loop(0, pairs, step, 0)
+        def by_row(i, carry):
+            for d in turns:
+                for k in range(2):
+                    row = i * 2 + cores[k]
+
+                    def go(row=row, d=d):
+                        act(cols[d] * nr + row, {"rows": row, "cols": cols[d]})
+
+                    if d == 0 and k == 0:
+                        pl.when(i != pair)(go)
+                    else:
+                        go()
+            return carry
+
+        lax.fori_loop(0, pairs, {"mixed": mixed, "far": far_first, "row": by_row}[how], 0)
 
     barrier = pltpu.get_barrier_semaphore()
-    to_all(lambda slot, device: pl.semaphore_signal(barrier, inc=1, device_id=device, device_id_type=MESH))
-
-    def send(src, dst, stride, base, rows, sem):
+    to_all(lambda slot, device: pl.semaphore_signal(barrier, inc=1, device_id=device, device_id_type=MESH), "far")
+
+    def send(src, dst, stride, base, rows, sem, how="mixed"):
         def act(slot, device):
             pltpu.make_async_remote_copy(
                 src_ref=src.at[pl.ds(slot * stride + base, rows)],
@@ -163,7 +196,7 @@
                 device_id_type=MESH,
             ).start()
 
-        to_all(act)
+        to_all(act, how)
         for q in range(rows):
             dst[pl.ds(me * stride + base + q, 1), :] = src[pl.ds(me * stride + base + q, 1), :]
 
@@ -265,8 +298,13 @@
         if a == 0:
             with jax.named_scope("barrier"):
                 pl.semaphore_wait(barrier, slots - 1)
+        at = 2 * groups * a
         with jax.named_scope("send_first"):
-            send(send_first, have_first, 2 * count, 2 * groups * a, 2 * groups, a)
+            if a < last:
+                send(send_first, have_first, 2 * count, at, 2 * groups, a)
+            else:
+                send(send_first, have_first, 2 * count, at, groups, a)
+                send(send_first, have_first, 2 * count, at + groups, groups, a + 1)
     for a in range(groups):
         gate = jax.nn.sigmoid(product(0, 4, 1, a * groups, groups))
         for b in range(groups):
@@ -288,7 +326,7 @@
                     pl.ds(b8 * SUB * ri + a * SUB + t, SUB, stride=ri), :
                 ]
 
-    def send_blocks(first, number, buffer, have, sem, strided):
+    def send_blocks(first, number, buffer, have, sem, strided, how="mixed"):
         for p in range(first, first + number):
             for b8 in range(half):
                 if strided:
@@ -296,7 +334,7 @@
                 else:
                     parts = [blocks[pl.ds(p * span + t * nr + b8 * SUB, SUB), :] for t in range(SUB)]
                 to_owners(parts, buffer, count, p, b8)
-        send(buffer, have, count, first, number, sem)
+        send(buffer, have, count, first, number, sem, how)
 
     def keep_blocks(values, firsts, seconds):
         for i, a in enumerate(firsts):
@@ -315,54 +353,73 @@
         )
         keep_blocks(values, firsts, seconds)
 
-    for a in range(groups):
-        with jax.named_scope("wait_first"):
-            await_bytes(have_first, 2 * groups, recv_sem, a)
+    def take_left(a):
+        rows = slice(a * span, (a + 1) * span)
         for b in range(groups):
             for b8 in range(half):
                 for t, part in enumerate(at_owner(have_first, 2 * count, 2 * groups * a + b, b8)):
                     rows_a[pl.ds(b * span + t * nr + b8 * SUB, SUB), :] = part
+        for b in range(groups):
+            high, low = high_low(rows_a[lanes_of(b), :] * mask_lanes[b, 0:1, :] * mask_far[rows, :])
+            left_cat[rows, lanes_of(b)] = high
+            left_cat[rows, lanes_of(groups + b)] = low
+            left_cat[rows, lanes_of(2 * groups + b)] = high
+
+    def take_right(a):
+        rows = slice(a * span, (a + 1) * span)
+        for b in range(groups):
+            for b8 in range(half):
                 for t, part in enumerate(at_owner(have_first, 2 * count, 2 * groups * a + groups + b, b8)):
                     rows_b[pl.ds(b * span + b8 * SUB * SUB + t, SUB, stride=SUB), :] = part
         for b in range(groups):
-            high, low = high_low(
-                rows_a[lanes_of(b), :] * mask_lanes[b, 0:1, :] * mask_far[a * span : (a + 1) * span, :]
-            )
-            rows = slice(a * span, (a + 1) * span)
-            left_cat[rows, lanes_of(b)] = high
-            left_cat[rows, lanes_of(groups + b)] = low
-            left_cat[rows, lanes_of(2 * groups + b)] = high
             high, low = high_low(rows_b[lanes_of(b), :] * mask_near[lanes_of(a), :])
             right_cat[rows, lanes_of(b)] = high
             right_cat[rows, lanes_of(groups + b)] = high
             right_cat[rows, lanes_of(2 * groups + b)] = low
-        if a == last - 1:
-            far_times_near(near_groups, near_groups)
-            with jax.named_scope("send_mixed"):
-                send_blocks(0, cut_a, send_mixed, have_mixed, groups, False)
+
+    def await_first(rows, sem):
+        with jax.named_scope("wait_first"):
+            await_bytes(have_first, rows, recv_sem, sem)
+
+    def send_mixed_tiles(first, stop, sem):
+        with jax.named_scope("send_mixed"):
+            send_blocks(first, stop - first, send_mixed, have_mixed, sem, False)
+
+    for a in range(last):
+        await_first(2 * groups, a)
+        take_left(a)
+        take_right(a)
+    far_times_near(near_groups, near_groups)
+    send_mixed_tiles(0, cut_a, groups + 1)
+    await_first(groups, last)
+    take_left(last)
     far_times_near([last], near_groups)
+    send_mixed_tiles(cut_a, cut_b, groups + 2)
+    await_first(groups, groups)
+    take_right(last)
     far_times_near(all_groups, [last])
-    with jax.named_scope("send_mixed"):
-        send_blocks(cut_a, count - cut_a, send_mixed, have_mixed, groups + 1, False)
-
-    def project_second(first, number, sem):
-        side(1, 0, 0, number, send_second, 2 * count, 2 * first)
-        side(1, 2, 0, number, send_second, 2 * count, 2 * first + number)
-        with jax.named_scope("send_second"):
-            send(send_second, have_second, 2 * count, 2 * first, 2 * number, sem)
-        gating[:, lanes_of(first, number)] = jax.nn.sigmoid(product(1, 4, 1, 0, number))
-
-    second_sets = ((0, cut_a), (cut_a, cut_b), (cut_b, count))
-    for i, (first, stop) in enumerate(second_sets):
+    send_mixed_tiles(cut_b, count, groups + 3)
+
+    sets = ((0, cut_a), (cut_a, cut_b), (cut_b, count))
+    for i, (first, stop) in enumerate(sets):
         number = stop - first
-        if i < 2:
-            with jax.named_scope("wait_mixed"):
-                await_bytes(have_mixed, (cut_a, count - cut_a)[i], recv_sem, groups + i)
+        with jax.named_scope("wait_mixed"):
+            await_bytes(have_mixed, number, recv_sem, groups + 1 + i)
         values = finish(0, first, number, have_mixed)
         state[:, lanes_of(first, number)] = values
         for t in range(number):
             normalize_into(state[:, lanes_of(first + t)], 1, t, 0)
-        project_second(first, number, groups + 2 + i)
+        side(1, 0, 0, number, send_second, 2 * count, 2 * first)
+        if i == 2:
+            with jax.named_scope("send_second"):
+                send(send_second, have_second, 2 * count, 2 * first, number, groups + 4 + i)
+        side(1, 2, 0, number, send_second, 2 * count, 2 * first + number)
+        with jax.named_scope("send_second"):
+            if i == 2:
+                send(send_second, have_second, 2 * count, 2 * first + number, number, groups + 5 + i)
+            else:
+                send(send_second, have_second, 2 * count, 2 * first, 2 * number, groups + 4 + i)
+        gating[:, lanes_of(first, number)] = jax.nn.sigmoid(product(1, 4, 1, 0, number))
 
     def under_times(firsts, seconds):
         values = jnp.dot(
@@ -372,53 +429,73 @@
         )
         keep_blocks(values, firsts, seconds)
 
-    for i, (first, stop) in enumerate(second_sets):
-        number = stop - first
-        with jax.named_scope("wait_second"):
-            await_bytes(have_second, 2 * number, recv_sem, groups + 2 + i)
+    def take_under_left(first, stop):
         for p in range(first, stop):
             a, b = order[p]
-            row = first + p
             for b8 in range(half):
-                for t, part in enumerate(at_owner(have_second, 2 * count, row, b8)):
+                for t, part in enumerate(at_owner(have_second, 2 * count, first + p, b8)):
                     rows_a[pl.ds(t * nr + b8 * SUB, SUB), :] = part
-                for t, part in enumerate(at_owner(have_second, 2 * count, row + number, b8)):
-                    rows_b[pl.ds(t * nr + b8 * SUB, SUB), :] = part
             high, low = high_low((rows_a[0:span, :] * mask_lanes[b, 0:1, :]).T)
             rows = slice(b * span, (b + 1) * span)
             left_cat[rows, lanes_of(a)] = high
             left_cat[rows, lanes_of(groups + a)] = low
             left_cat[rows, lanes_of(2 * groups + a)] = high
+
+    def take_under_right(first, stop):
+        for p in range(first, stop):
+            a, b = order[p]
+            for b8 in range(half):
+                for t, part in enumerate(at_owner(have_second, 2 * count, p + stop, b8)):
+                    rows_b[pl.ds(t * nr + b8 * SUB, SUB), :] = part
             high, low = high_low(
                 rows_b[0:span, :] * mask_lanes[b, 0:1, :] * mask_far[a * span : (a + 1) * span, :]
             )
             under_cat[lanes_of(a), lanes_of(b)] = high
             under_cat[lanes_of(groups + a), lanes_of(b)] = high
             under_cat[lanes_of(2 * groups + a), lanes_of(b)] = low
-        if i == 1:
-            under_times(near_groups, near_groups)
-            with jax.named_scope("send_next"):
-                send_blocks(0, cut_a, send_next, have_next, groups + 5, True)
+
+    def await_second(rows, sem):
+        with jax.named_scope("wait_second"):
+            await_bytes(have_second, rows, recv_sem, sem)
+
+    def send_next_tiles(first, stop, sem, how):
+        with jax.named_scope("send_next"):
+            send_blocks(first, stop - first, send_next, have_next, sem, True, how)
+
+    for i in range(2):
+        first, stop = sets[i]
+        await_second(2 * (stop - first), groups + 4 + i)
+        take_under_left(first, stop)
+        take_under_right(first, stop)
+    under_times(near_groups, near_groups)
+    send_next_tiles(0, cut_a, groups + 8, "mixed")
+    await_second(groups, groups + 6)
+    take_under_left(cut_b, count)
     under_times([last], near_groups)
+    send_next_tiles(cut_a, cut_b, groups + 9, "row")
+    await_second(groups, groups + 7)
+    take_under_right(cut_b, count)
     under_times(all_groups, [last])
-    with jax.named_scope("send_next"):
-        send_blocks(cut_a, count - cut_a, send_next, have_next, groups + 6, True)
-    for i, (first, stop) in enumerate(((0, cut_a), (cut_a, count))):
+    send_next_tiles(cut_b, count, groups + 10, "row")
+    for i, (first, stop) in enumerate(sets):
         with jax.named_scope("wait_next"):
-            await_bytes(have_next, stop - first, recv_sem, groups + 5 + i)
+            await_bytes(have_next, stop - first, recv_sem, groups + 8 + i)
         values = finish(1, first, stop - first, have_next)
         for p in range(first, stop):
             tile = values[:, lanes_of(p - first)].T
             for q, rows in enumerate(pieces(p)):
                 y_ref[rows, :] = tile[q * SUB : (q + 1) * SUB, :]
 
-    for a in range(groups):
+    for a in range(last):
         await_bytes(send_first, 2 * groups, send_sem, a)
-    for i, rows in enumerate((cut_a, count - cut_a)):
-        await_bytes(send_mixed, rows, send_sem, groups + i)
-        await_bytes(send_next, rows, send_sem, groups + 5 + i)
-    for i, (first, stop) in enumerate(second_sets):
-        await_bytes(send_second, 2 * (stop - first), send_sem, groups + 2 + i)
+    for part in range(2):
+        await_bytes(send_first, groups, send_sem, last + part)
+        await_bytes(send_second, groups, send_sem, groups + 6 + part)
+    for i, (first, stop) in enumerate(sets):
+        await_bytes(send_mixed, stop - first, send_sem, groups + 1 + i)
+        await_bytes(send_next, stop - first, send_sem, groups + 8 + i)
+        if i < 2:
+            await_bytes(send_second, 2 * (stop - first), send_sem, groups + 4 + i)
 
 
 def body(
@@ -488,8 +565,8 @@
             pltpu.VMEM((3 * tokens, tokens), BF16),
             pltpu.VMEM((count * LANES, LANES), F32),
             pltpu.SemaphoreType.DMA((len(inputs),)),
-            pltpu.SemaphoreType.DMA((groups + 7,)),
-            pltpu.SemaphoreType.DMA((groups + 7,)),
+            pltpu.SemaphoreType.DMA((groups + 11,)),
+            pltpu.SemaphoreType.DMA((groups + 11,)),
         ],
         compiler_params=pltpu.CompilerParams(
             collective_id=0, has_side_effects=True, vmem_limit_bytes=48 * 2**20

time: 109 us -> 106 us (0.972)
  Pallas kernels: 108 us -> 105 us
    pallas_call x1, Pallas kernels: 108 us -> 105 us  [body(): pl.pallas_call(functools.partial(kernel, (nr, nc, ri, cj)), out_shape=jax...]
where the time goes in v3:
time: 106 us
  Pallas kernels  105 us (99%)
    pallas_call x1, Pallas kernels, body(): pl.pallas_call(functools.partial(kernel, (nr, nc, ri, cj)), out_shape=jax...  105 us

profile of v3, /device:TPU:513, one launch (start us, length us, event | category | flops | bytes accessed | tf_op | source)
XLA Modules:
  0.0 105.8 jit_solution(6925049863164557238)
XLA Ops:
  0.0 105.0 %triangles.1 = f32[1152,128]{1,0:T(8,128)S(1)} custom-call(f32[1152,128]{1,0:T(8,128)} %bitcast.4, s32[3,128]{1,0:T(4,128)} %bitcast.5, f32[2,128]{1,0:T(2,128)} %norm_gain_hbm.1, f32[2,128]{1,0:T(2,128)} %norm_bias_hbm.1, f32[2,128,512]{2,1,0:T(8,128)} %proj_hbm.1, f32[2,128,128]{2,1,0:T(8,128)} %gate_hbm.1, f32[2,128]{1,0:T(2,128)} %out_gain_hbm.1, ...), custom_call_target="tpu_custom_call" | custom-call | tf_op jit(solution)/shard_map/triangles/pallas_call | solution.py:537
  105.0 0.8 copy.11

commit v4 on v3

--- a/solution.py
+++ b/solution.py
@@ -86,6 +86,7 @@
     load_sem,
     send_sem,
     recv_sem,
+    ready,
 ):
     nr, nc, ri, cj = sizes
     slots = nr * nc
@@ -183,9 +184,22 @@
         lax.fori_loop(0, pairs, {"mixed": mixed, "far": far_first, "row": by_row}[how], 0)
 
     barrier = pltpu.get_barrier_semaphore()
-    to_all(lambda slot, device: pl.semaphore_signal(barrier, inc=1, device_id=device, device_id_type=MESH), "far")
-
-    def send(src, dst, stride, base, rows, sem, how="mixed"):
+
+    def greet(semaphore):
+        to_all(
+            lambda slot, device: pl.semaphore_signal(semaphore, inc=1, device_id=device, device_id_type=MESH), "far"
+        )
+
+    @pl.when(me != 0)
+    def _():
+        greet(barrier)
+
+    @pl.when(me == 0)
+    def _():
+        pl.semaphore_wait(barrier, slots - 1)
+        greet(ready)
+
+    def copy_to(src, dst, stride, base, rows, sem):
         def act(slot, device):
             pltpu.make_async_remote_copy(
                 src_ref=src.at[pl.ds(slot * stride + base, rows)],
@@ -196,9 +210,15 @@
                 device_id_type=MESH,
             ).start()
 
-        to_all(act, how)
+        return act
+
+    def keep_own(src, dst, stride, base, rows):
         for q in range(rows):
             dst[pl.ds(me * stride + base + q, 1), :] = src[pl.ds(me * stride + base + q, 1), :]
+
+    def send(src, dst, stride, base, rows, sem, how="mixed"):
+        to_all(copy_to(src, dst, stride, base, rows, sem), how)
+        keep_own(src, dst, stride, base, rows)
 
     def await_bytes(buffer, rows, sems, sem):
         whole = buffer.at[pl.ds(0, (slots - 1) * rows)]
@@ -295,10 +315,24 @@
             normalize_into(values, 0, a * groups + b, 0)
         side(0, 0, a * groups, groups, send_first, 2 * count, 2 * groups * a)
         side(0, 2, a * groups, groups, send_first, 2 * count, 2 * groups * a + groups)
+        at = 2 * groups * a
         if a == 0:
-            with jax.named_scope("barrier"):
-                pl.semaphore_wait(barrier, slots - 1)
-        at = 2 * groups * a
+            with jax.named_scope("send_first"):
+                copy = copy_to(send_first, have_first, 2 * count, at, 2 * groups, a)
+
+                @pl.when(me == 0)
+                def _():
+                    to_all(copy, "mixed")
+
+                @pl.when(me != 0)
+                def _():
+                    pl.semaphore_wait(barrier, slots - 2)
+                    to_all(lambda slot, device: pl.when(slot != 0)(lambda: copy(slot, device)), "mixed")
+                    pl.semaphore_wait(ready, 1)
+                    copy(0, {"rows": 0, "cols": 0})
+
+                keep_own(send_first, have_first, 2 * count, at, 2 * groups)
+            continue
         with jax.named_scope("send_first"):
             if a < last:
                 send(send_first, have_first, 2 * count, at, 2 * groups, a)
@@ -567,6 +601,7 @@
             pltpu.SemaphoreType.DMA((len(inputs),)),
             pltpu.SemaphoreType.DMA((groups + 11,)),
             pltpu.SemaphoreType.DMA((groups + 11,)),
+            pltpu.SemaphoreType.REGULAR,
         ],
         compiler_params=pltpu.CompilerParams(
             collective_id=0, has_side_effects=True, vmem_limit_bytes=48 * 2**20

time: 106 us -> 104 us (0.981)
  Pallas kernels: 105 us -> 103 us
    pallas_call x1, Pallas kernels: 105 us -> 103 us  [body(): pl.pallas_call(functools.partial(kernel, (nr, nc, ri, cj)), out_shape=jax...]
where the time goes in v4:
time: 104 us
  Pallas kernels  103 us (99%)
    pallas_call x1, Pallas kernels, body(): pl.pallas_call(functools.partial(kernel, (nr, nc, ri, cj)), out_shape=jax...  103 us

profile of v4, /device:TPU:513, one launch (start us, length us, event | category | flops | bytes accessed | tf_op | source)
XLA Modules:
  0.0 104.2 jit_solution(4516338694720487779)
XLA Ops:
  0.0 103.4 %triangles.1 = f32[1152,128]{1,0:T(8,128)S(1)} custom-call(f32[1152,128]{1,0:T(8,128)} %bitcast.4, s32[3,128]{1,0:T(4,128)} %bitcast.5, f32[2,128]{1,0:T(2,128)} %norm_gain_hbm.1, f32[2,128]{1,0:T(2,128)} %norm_bias_hbm.1, f32[2,128,512]{2,1,0:T(8,128)} %proj_hbm.1, f32[2,128,128]{2,1,0:T(8,128)} %gate_hbm.1, f32[2,128]{1,0:T(2,128)} %out_gain_hbm.1, ...), custom_call_target="tpu_custom_call" | custom-call | tf_op jit(solution)/shard_map/triangles/pallas_call | solution.py:571
  103.4 0.8 copy.11

commit v5 on v4

--- a/solution.py
+++ b/solution.py
@@ -168,7 +168,7 @@
             return carry
 
         def by_row(i, carry):
-            for d in turns:
+            for d in sorted(turns, key=lambda d: -min(d, nc - d)):
                 for k in range(2):
                     row = i * 2 + cores[k]
 
@@ -450,7 +450,7 @@
         side(1, 2, 0, number, send_second, 2 * count, 2 * first + number)
         with jax.named_scope("send_second"):
             if i == 2:
-                send(send_second, have_second, 2 * count, 2 * first + number, number, groups + 5 + i)
+                send(send_second, have_second, 2 * count, 2 * first + number, number, groups + 5 + i, "far")
             else:
                 send(send_second, have_second, 2 * count, 2 * first, 2 * number, groups + 4 + i)
         gating[:, lanes_of(first, number)] = jax.nn.sigmoid(product(1, 4, 1, 0, number))
@@ -502,7 +502,7 @@
         take_under_left(first, stop)
         take_under_right(first, stop)
     under_times(near_groups, near_groups)
-    send_next_tiles(0, cut_a, groups + 8, "mixed")
+    send_next_tiles(0, cut_a, groups + 8, "far")
     await_second(groups, groups + 6)
     take_under_left(cut_b, count)
     under_times([last], near_groups)

time: 104 us -> 103 us (level)
    pallas_call x1, Pallas kernels: 103 us -> 102 us  [body(): pl.pallas_call(functools.partial(kernel, (nr, nc, ri, cj)), out_shape=jax...]
where the time goes in v5:
time: 103 us
  Pallas kernels  102 us (99%)
    pallas_call x1, Pallas kernels, body(): pl.pallas_call(functools.partial(kernel, (nr, nc, ri, cj)), out_shape=jax...  102 us

profile of v5, /device:TPU:513, one launch (start us, length us, event | category | flops | bytes accessed | tf_op | source)
XLA Modules:
  0.0 102.9 jit_solution(17462432584476553653)
XLA Ops:
  0.0 102.1 %triangles.1 = f32[1152,128]{1,0:T(8,128)S(1)} custom-call(f32[1152,128]{1,0:T(8,128)} %bitcast.4, s32[3,128]{1,0:T(4,128)} %bitcast.5, f32[2,128]{1,0:T(2,128)} %norm_gain_hbm.1, f32[2,128]{1,0:T(2,128)} %norm_bias_hbm.1, f32[2,128,512]{2,1,0:T(8,128)} %proj_hbm.1, f32[2,128,128]{2,1,0:T(8,128)} %gate_hbm.1, f32[2,128]{1,0:T(2,128)} %out_gain_hbm.1, ...), custom_call_target="tpu_custom_call" | custom-call | tf_op jit(solution)/shard_map/triangles/pallas_call | solution.py:571
  102.1 0.8 copy.11

commit v6 on v5

--- a/solution.py
+++ b/solution.py
@@ -338,7 +338,7 @@
                 send(send_first, have_first, 2 * count, at, 2 * groups, a)
             else:
                 send(send_first, have_first, 2 * count, at, groups, a)
-                send(send_first, have_first, 2 * count, at + groups, groups, a + 1)
+                send(send_first, have_first, 2 * count, at + groups, groups, a + 1, "far")
     for a in range(groups):
         gate = jax.nn.sigmoid(product(0, 4, 1, a * groups, groups))
         for b in range(groups):

time: 103 us -> 104 us (level)
  no operation moved by 1% of the time
where the time goes in v6:
time: 104 us
  Pallas kernels  103 us (99%)
    pallas_call x1, Pallas kernels, body(): pl.pallas_call(functools.partial(kernel, (nr, nc, ri, cj)), out_shape=jax...  103 us

profile of v6, /device:TPU:513, one launch (start us, length us, event | category | flops | bytes accessed | tf_op | source)
XLA Modules:
  0.0 103.8 jit_solution(7925876858656740664)
XLA Ops:
  0.0 102.9 %triangles.1 = f32[1152,128]{1,0:T(8,128)S(1)} custom-call(f32[1152,128]{1,0:T(8,128)} %bitcast.4, s32[3,128]{1,0:T(4,128)} %bitcast.5, f32[2,128]{1,0:T(2,128)} %norm_gain_hbm.1, f32[2,128]{1,0:T(2,128)} %norm_bias_hbm.1, f32[2,128,512]{2,1,0:T(8,128)} %proj_hbm.1, f32[2,128,128]{2,1,0:T(8,128)} %gate_hbm.1, f32[2,128]{1,0:T(2,128)} %out_gain_hbm.1, ...), custom_call_target="tpu_custom_call" | custom-call | tf_op jit(solution)/shard_map/triangles/pallas_call | solution.py:571
  102.9 0.8 copy.11

commit v7 on v5

--- a/solution.py
+++ b/solution.py
@@ -446,7 +446,7 @@
         side(1, 0, 0, number, send_second, 2 * count, 2 * first)
         if i == 2:
             with jax.named_scope("send_second"):
-                send(send_second, have_second, 2 * count, 2 * first, number, groups + 4 + i)
+                send(send_second, have_second, 2 * count, 2 * first, number, groups + 4 + i, "far")
         side(1, 2, 0, number, send_second, 2 * count, 2 * first + number)
         with jax.named_scope("send_second"):
             if i == 2:

time: 103 us -> 103 us (level)
  no operation moved by 1% of the time
where the time goes in v7:
time: 103 us
  Pallas kernels  102 us (99%)
    pallas_call x1, Pallas kernels, body(): pl.pallas_call(functools.partial(kernel, (nr, nc, ri, cj)), out_shape=jax...  102 us

profile of v7, /device:TPU:513, one launch (start us, length us, event | category | flops | bytes accessed | tf_op | source)
XLA Modules:
  0.0 103.0 jit_solution(13175328760553385806)
XLA Ops:
  0.0 102.1 %triangles.1 = f32[1152,128]{1,0:T(8,128)S(1)} custom-call(f32[1152,128]{1,0:T(8,128)} %bitcast.4, s32[3,128]{1,0:T(4,128)} %bitcast.5, f32[2,128]{1,0:T(2,128)} %norm_gain_hbm.1, f32[2,128]{1,0:T(2,128)} %norm_bias_hbm.1, f32[2,128,512]{2,1,0:T(8,128)} %proj_hbm.1, f32[2,128,128]{2,1,0:T(8,128)} %gate_hbm.1, f32[2,128]{1,0:T(2,128)} %out_gain_hbm.1, ...), custom_call_target="tpu_custom_call" | custom-call | tf_op jit(solution)/shard_map/triangles/pallas_call | solution.py:571
  102.2 0.8 copy.11
